TPU v7x, 256 devices: a whole 4x4x8 slice. The times are simulated.
256 devices in a mesh: arcs: 2 (over z_lo), trow: 8 (over y, core), tcol: 16 (over x, z_hi).
Axes of the slice: x: 4, y: 4, z: 8 (z_hi: 4, z_lo: 2; z = z_hi * 2 + z_lo), core: 2. Of those that a mesh axis runs over, the one named last changes fastest.
Arguments:
- design: bfloat16 [4096, 12288], P(('arcs', 'tcol'), 'trow'), may hold values from -6 to 6
- observed: float32 [4096], P(('arcs', 'tcol')), may hold values from -6 to 6
- arc_counts: int32 [128], P(('arcs', 'tcol')), may hold values from 2 to 32
- arc_weight: float32 [128], P(('arcs', 'tcol')), may hold values from 0.3 to 3
Outputs:
- gram: float32 [12288, 12288], P('trow', ('arcs', 'tcol'))
- rhs: float32 [12288], P('trow')
Inputs may be any that keep to these rules, and one draw needn't show every extreme that they name: `arc_counts`: each arc has at least two valid observations.
All inputs are finite; a program needn't handle non-finite values.
Results may differ from a plain program's by a relative error of at most 0.0055.
Values may be sent and summed in bfloat16 or wider, within the bound.
No kernel may reach another device: no remote copies, remote signals or barrier semaphores. Data moves between devices by JAX's collectives and lax.ppermute only.
A program may use at most 192 MiB of HBM per device.

v0:
```python
import jax
import jax.numpy as jnp
from jax import lax
from jax.sharding import PartitionSpec as P


def from_everyone(x, axis):
    devices = lax.axis_size(axis)
    return lax.all_to_all(jnp.broadcast_to(x[None], (devices, *x.shape)), axis, 0, 0, tiled=True)


def over_copies(x, axis):
    return from_everyone(x, axis).sum(axis=0)


def cut_along(x, dim, devices):
    dims = x.shape
    blocks = x.reshape(*dims[:dim], devices, dims[dim] // devices, *dims[dim + 1 :])
    return jnp.moveaxis(blocks, dim, 0)


def sum_at_owner(x, axis, dim):
    blocks = cut_along(x, dim, lax.axis_size(axis))
    arrived = lax.all_to_all(blocks, axis, split_axis=0, concat_axis=0, tiled=True)
    return arrived.astype(jnp.float32).sum(axis=0)


def fold_with(right, piece):
    return lax.dot_general(
        piece, right, (((0,), (0,)), ((), ())), preferred_element_type=jnp.float32
    )


def local(design, observed, arc_counts, arc_weight):
    row_count, col_width = design.shape
    arc_total = arc_counts.shape[0]
    arc_len = row_count // arc_total
    slot_index = lax.broadcasted_iota(jnp.int32, (arc_total, arc_len), 1)
    valid_mask = (slot_index < arc_counts[:, None]).astype(jnp.float32)
    counts_float = arc_counts.astype(jnp.float32)
    factor = valid_mask * jnp.sqrt(arc_weight)[:, None]
    blocks = design.reshape(arc_total, arc_len, col_width).astype(jnp.float32)
    column_mean = jnp.sum(valid_mask[:, :, None] * blocks, axis=1) / counts_float[:, None]
    centered = (
        (factor[:, :, None] * (blocks - column_mean[:, None, :]))
        .reshape(row_count, col_width)
        .astype(jnp.bfloat16)
    )
    series = observed.reshape(arc_total, arc_len)
    series_mean = jnp.sum(valid_mask * series, axis=1) / counts_float
    weighted = (factor * (series - series_mean[:, None])).reshape(row_count)
    arc_devices = lax.axis_size("arcs")
    tcol_devices = lax.axis_size("tcol")
    obs_total = row_count * arc_devices * tcol_devices
    rhs_part = jnp.dot(weighted, centered.astype(jnp.float32), precision=lax.Precision.HIGHEST)
    rhs = over_copies(rhs_part, ("arcs", "tcol")) * obs_total ** (-0.5)
    every_coef = lax.all_gather(centered, "trow", axis=1, tiled=True)
    full_width = every_coef.shape[1]
    narrow = full_width // (arc_devices * tcol_devices)
    shaped = every_coef.reshape(row_count, arc_devices, tcol_devices, narrow)
    moved = lax.all_to_all(shaped, "tcol", split_axis=2, concat_axis=0, tiled=True)
    right = moved.reshape(row_count * tcol_devices, arc_devices * narrow)
    partial_value = fold_with(right, lax.all_gather(centered, "tcol", axis=0, tiled=True))
    tile = sum_at_owner(partial_value.astype(jnp.bfloat16), "arcs", 1)
    gram = tile * (1.0 / obs_total)
    return (gram, rhs)


def solution(mesh):
    return jax.shard_map(
        local,
        mesh=mesh,
        in_specs=(
            P(("arcs", "tcol"), "trow"),
            P(("arcs", "tcol")),
            P(("arcs", "tcol")),
            P(("arcs", "tcol")),
        ),
        out_specs=(P("trow", ("arcs", "tcol")), P("trow")),
        check_vma=False,
    )
```

profile of v0, /device:TPU:1, one launch (start us, length us, event | category | flops | bytes accessed | tf_op | source)
XLA Modules:
  0.0 264.2 jit_solution(5195800618479505239)
XLA Ops:
  7.2 0.0 all-gather.5.cloned.1.call-start
  7.2 0.7 fusion.4
  7.9 0.7 convert_element_type.33
  8.6 0.7 reshape.101
  9.3 0.7 sqrt.3
  10.0 1.4 select_reduce_fusion
  11.3 0.1 mul.48
  11.4 1.2 multiply_reduce_fusion
  12.6 0.1 broadcast_divide_fusion
  12.7 1.9 fusion.3
  14.6 0.0 all-gather.5.cloned.1.call-update
  14.6 0.0 all-gather.3.cloned.1.call-start
  14.6 0.7 all-gather.3.cloned.1.call-update
  15.3 33.9 %all-gather.5.cloned.1.call-done = bf16[128,12288]{1,0:T(8,128)(2,1)} async-done(((bf16[128,1536]{1,0:T(8,128)(2,1)}), bf16[128,12288]{1,0:T(8,128)(2,1)}) %all-gather.5.cloned.1.call-update) | async-done | bytes 3145744 | tf_op jit(solution)/shard_map/all_gather | solution.py:57
  49.2 3.5 %copy.21 = bf16[128,12288]{0,1:T(8,128)(2,1)S(1)} copy(bf16[128,12288]{1,0:T(8,128)(2,1)} %all-gather.5.cloned.1.call-done) | data formatting | bytes 6291456 | tf_op jit(solution)/shard_map/all_gather | solution.py:57
  52.7 1.9 copy.22
  54.6 0.0 copy-start.2
  54.6 0.0 copy-start
  54.6 0.0 copy-start.1
  54.6 9.4 %all-to-all-start = ((bf16[128,2,16,384]{0,3,1,2:T(8,128)(2,1)}), bf16[128,2,16,384]{0,3,1,2:T(8,128)(2,1)S(1)}, u32[]{:S(2)}, u32[]{:S(2)}) async-start(bf16[128,2,16,384]{0,3,1,2:T(8,128)(2,1)} %copy.22), calls=%async_computation | async-start | bytes 6291456 | tf_op jit(solution)/shard_map/all_to_all | solution.py:61
  64.0 0.0 copy-done.2
  64.0 0.7 convert_divide_fusion
  64.7 0.1 sub.25
  64.7 0.6 sub.26
  65.3 0.0 copy-done
  65.3 0.0 copy-done.1
  65.3 0.9 convolution_reduce_fusion
  66.3 82.1 %all-to-all-done = bf16[128,2,16,384]{0,3,1,2:T(8,128)(2,1)S(1)} async-done(((bf16[128,2,16,384]{0,3,1,2:T(8,128)(2,1)}), bf16[128,2,16,384]{0,3,1,2:T(8,128)(2,1)S(1)}, u32[]{:S(2)}, u32[]{:S(2)}) %all-to-all-start) | async-done | bytes 3145760 | tf_op jit(solution)/shard_map/all_to_all | solution.py:61
  148.4 0.8 broadcast_in_dim.2
  149.2 10.1 %all-to-all-start.2 = ((f32[32,1,1536]{2,1,0:T(1,128)}), f32[32,1,1536]{2,1,0:T(1,128)S(1)}, u32[]{:S(2)}, u32[]{:S(2)}) async-start(f32[32,1,1536]{2,1,0:T(1,128)} %broadcast_in_dim.2), calls=%async_computation.2 | async-start | bytes 393216 | tf_op jit(solution)/shard_map/all_to_all | solution.py:9
  159.2 3.7 %copy.23 = bf16[16,128,2,1,384]{1,0,4,2,3:T(8,128)(2,1)} copy(bf16[16,128,2,1,384]{1,4,2,0,3:T(8,128)(2,1)S(1)} %bitcast.27) | data formatting | bytes 6291456 | tf_op jit(solution)/shard_map/all_to_all | solution.py:61
  163.0 51.0 %all-gather.3.cloned.1.call-done = bf16[2048,1536]{1,0:T(8,128)(2,1)} async-done(((bf16[128,1536]{1,0:T(8,128)(2,1)}), bf16[2048,1536]{1,0:T(8,128)(2,1)}) %all-gather.3.cloned.1.call-update) | async-done | bytes 6291472 | tf_op jit(solution)/shard_map/all_gather | solution.py:63
  213.9 9.5 %convolution_convert_fusion = bf16[1536,768]{0,1:T(8,128)(2,1)} fusion(bf16[2048,1536]{1,0:T(8,128)(2,1)} %all-gather.3.cloned.1.call-done, bf16[96,8,16,128]{3,2,1,0:T(8,128)(2,1)} %bitcast.29), kind=kOutput, calls=%fused_computation.1 | convolution fusion | flops 4833017856 | bytes 11796480 | tf_op jit(solution)/shard_map/dot_general | solution.py:29
  223.4 0.0 all-to-all-done.2
  223.4 3.8 %all-to-all-start.1 = ((bf16[2,1536,384]{1,2,0:T(8,128)(2,1)}), bf16[2,1536,384]{1,2,0:T(8,128)(2,1)S(1)}, u32[]{:S(2)}, u32[]{:S(2)}) async-start(bf16[2,1536,384]{1,2,0:T(8,128)(2,1)} %bitcast.30), calls=%async_computation.1 | async-start | bytes 4718592 | tf_op jit(solution)/shard_map/all_to_all | solution.py:24
  227.3 0.1 reduce_sum.39
  227.4 0.6 broadcast_multiply_fusion.1
  228.0 26.8 %all-to-all-done.1 = bf16[2,1536,384]{1,2,0:T(8,128)(2,1)S(1)} async-done(((bf16[2,1536,384]{1,2,0:T(8,128)(2,1)}), bf16[2,1536,384]{1,2,0:T(8,128)(2,1)S(1)}, u32[]{:S(2)}, u32[]{:S(2)}) %all-to-all-start.1) | async-done | bytes 2359328 | tf_op jit(solution)/shard_map/all_to_all | solution.py:24
  254.8 0.4 convert_reduce_fusion
  255.2 0.2 broadcast_multiply_fusion
  255.4 2.0 copy.25
Async XLA Ops:
  7.2 42.0 %all-gather.5.cloned.1.call-start = ((), (), s32[]{:S(2)}) async-start(), calls=%async_computation.4 | async-start | bytes 3538944 | tf_op jit(solution)/shard_map/all_gather | solution.py:57
  14.6 199.3 %all-gather.3.cloned.1.call-start = ((), (), s32[]{:S(2)}) async-start(), calls=%async_computation.3 | async-start | bytes 6684672 | tf_op jit(solution)/shard_map/all_gather | solution.py:63
  54.6 9.4 %copy-start.2 = (s32[4]{0:T(128)S(1)}, s32[4]{0:T(128)}, u32[]{:S(2)}) copy-start(s32[4]{0:T(128)} %param.6) | copy-start | bytes 52
  54.6 10.7 %copy-start = (bf16[128,1536]{1,0:T(8,128)(2,1)S(1)}, bf16[128,1536]{1,0:T(8,128)(2,1)}, u32[]{:S(2)}) copy-start(bf16[128,1536]{1,0:T(8,128)(2,1)} %fusion.3) | copy-start | bytes 1179652
  54.6 10.7 %copy-start.1 = (f32[128]{0:T(128)S(1)}, f32[128]{0:T(128)}, u32[]{:S(2)}) copy-start(f32[128]{0:T(128)} %param.5) | copy-start | bytes 1540
  54.6 93.8 %all-to-all-start = ((bf16[128,2,16,384]{0,3,1,2:T(8,128)(2,1)}), bf16[128,2,16,384]{0,3,1,2:T(8,128)(2,1)S(1)}, u32[]{:S(2)}, u32[]{:S(2)}) async-start(bf16[128,2,16,384]{0,3,1,2:T(8,128)(2,1)} %copy.22), calls=%async_computation | async-start | bytes 6291456 | tf_op jit(solution)/shard_map/all_to_all | solution.py:61
  149.2 74.3 %all-to-all-start.2 = ((f32[32,1,1536]{2,1,0:T(1,128)}), f32[32,1,1536]{2,1,0:T(1,128)S(1)}, u32[]{:S(2)}, u32[]{:S(2)}) async-start(f32[32,1,1536]{2,1,0:T(1,128)} %broadcast_in_dim.2), calls=%async_computation.2 | async-start | bytes 393216 | tf_op jit(solution)/shard_map/all_to_all | solution.py:9
  223.4 31.3 %all-to-all-start.1 = ((bf16[2,1536,384]{1,2,0:T(8,128)(2,1)}), bf16[2,1536,384]{1,2,0:T(8,128)(2,1)S(1)}, u32[]{:S(2)}, u32[]{:S(2)}) async-start(bf16[2,1536,384]{1,2,0:T(8,128)(2,1)} %bitcast.30), calls=%async_computation.1 | async-start | bytes 4718592 | tf_op jit(solution)/shard_map/all_to_all | solution.py:24
Sparse Core Ops, SparseCore 0:
  14.7 34.4 all-gather.4
  52.2 161.6 all-gather.2
where the time goes:
time: 265 us; the launch traced here: 264 us
  waiting for transfers between devices  194 us (73%)
  starting transfers between devices  23.3 us (9%)
  between operations  14.1 us (5%)
  local copies, waits for them, and re-layouts  14 us (5%)
  matrix products  10.4 us (4%)
  other arithmetic  7.85 us (3%)
    all_to_all x1, waiting for transfers between devices, local(): lax.all_to_all(shaped, 'tcol', split_axis=2, concat_axis=0, tiled=True)  82.1 us
    all_gather x1, waiting for transfers between devices, local(): lax.all_gather(centered, 'tcol', axis=0, tiled=True)  51 us
    all_gather x1, waiting for transfers between devices, local(): every_coef = lax.all_gather(centered, 'trow', axis=1, tiled=True)  33.9 us
    all_to_all x1, waiting for transfers between devices, sum_at_owner(): lax.all_to_all(blocks, axis, split_axis=0, concat_axis=0, tiled=True)  26.8 us
    all_to_all x1, starting transfers between devices, from_everyone(): lax.all_to_all(jnp.broadcast_to(x[None], (devices, *x.shape)), axis, 0, 0...  10.1 us
    dot_general x1, matrix products, fold_with(): lax.dot_general(piece, right, (((0,), (0,)), ((), ())), preferred_element...  9.51 us
    all_to_all x1, starting transfers between devices, local(): lax.all_to_all(shaped, 'tcol', split_axis=2, concat_axis=0, tiled=True)  9.38 us
  transfers between devices with their start and end apart: 5, of which 4 were waited for; matrix products, arithmetic and copies ran while one was open for 8% of the time, Pallas kernels for 0%

commit v1 on v0

--- a/solution.py
+++ b/solution.py
@@ -2,6 +2,13 @@
 import jax.numpy as jnp
 from jax import lax
 from jax.sharding import PartitionSpec as P
+
+
+def swapped_in(shard, axis, dim):
+    size = lax.axis_size(axis)
+    tiles = jnp.stack([shard for _ in range(size)])
+    tiles = lax.all_to_all(tiles, axis, split_axis=0, concat_axis=0)
+    return jnp.concatenate(tiles, axis=dim)
 
 
 def from_everyone(x, axis):
@@ -60,7 +67,7 @@
     shaped = every_coef.reshape(row_count, arc_devices, tcol_devices, narrow)
     moved = lax.all_to_all(shaped, "tcol", split_axis=2, concat_axis=0, tiled=True)
     right = moved.reshape(row_count * tcol_devices, arc_devices * narrow)
-    partial_value = fold_with(right, lax.all_gather(centered, "tcol", axis=0, tiled=True))
+    partial_value = fold_with(right, swapped_in(centered, "tcol", 0))
     tile = sum_at_owner(partial_value.astype(jnp.bfloat16), "arcs", 1)
     gram = tile * (1.0 / obs_total)
     return (gram, rhs)

time: 265 us -> 345 us (1.30)
  blocking collectives: 0 us -> 82.9 us
  starting transfers between devices: 23.3 us -> 15.2 us
    all_to_all x0 -> x1, blocking collectives: none -> 82.9 us  [local(): lax.all_to_all(shaped, 'tcol', split_axis=2, concat_axis=0, tiled=True)]
    all_to_all x1, waiting for transfers between devices: 82.1 us -> 137 us  [swapped_in(): tiles = lax.all_to_all(tiles, axis, split_axis=0, concat_axis=0)]
    all_gather x1 -> x0, waiting for transfers between devices: 51 us -> none  [local(): lax.all_gather(centered, 'tcol', axis=0, tiled=True)]
    all_to_all x1, starting transfers between devices: 9.38 us -> 4.76 us  [swapped_in(): tiles = lax.all_to_all(tiles, axis, split_axis=0, concat_axis=0)]
  transfers between devices with their start and end apart: 5 -> 4, of which waited for: 4 -> 4; matrix products, arithmetic and copies ran while one was open for 8% -> 5% of each run, Pallas kernels for 0% -> 0%
where the time goes in v1:
time: 345 us; the launch traced here: 342 us
  waiting for transfers between devices  196 us (57%)
  blocking collectives  82.9 us (24%)
  local copies, waits for them, and re-layouts  15.5 us (4%)
  starting transfers between devices  15.2 us (4%)
  between operations  14.1 us (4%)
  matrix products  10.5 us (3%)
  other arithmetic  7.84 us (2%)
    all_to_all x1, waiting for transfers between devices, swapped_in(): tiles = lax.all_to_all(tiles, axis, split_axis=0, concat_axis=0)  137 us
    all_to_all x1, blocking collectives, local(): lax.all_to_all(shaped, 'tcol', split_axis=2, concat_axis=0, tiled=True)  82.9 us
    all_gather x1, waiting for transfers between devices, local(): every_coef = lax.all_gather(centered, 'trow', axis=1, tiled=True)  34.6 us
    all_to_all x1, waiting for transfers between devices, sum_at_owner(): lax.all_to_all(blocks, axis, split_axis=0, concat_axis=0, tiled=True)  24.5 us
    dot_general x1, matrix products, fold_with(): lax.dot_general(piece, right, (((0,), (0,)), ((), ())), preferred_element...  9.53 us
  transfers between devices with their start and end apart: 4, of which 4 were waited for; matrix products, arithmetic and copies ran while one was open for 5% of the time, Pallas kernels for 0%

profile of v1, /device:TPU:1, one launch (start us, length us, event | category | flops | bytes accessed | tf_op | source)
XLA Modules:
  0.0 342.4 jit_solution(2318760989688209803)
XLA Ops:
  7.2 0.0 all-gather.2.cloned.1.call-start
  7.2 0.7 fusion.4
  7.9 0.7 convert_element_type.33
  8.6 0.7 reshape.107
  9.3 0.7 sqrt.3
  10.0 1.4 select_reduce_fusion
  11.3 0.1 mul.48
  11.4 1.2 multiply_reduce_fusion
  12.6 0.1 broadcast_divide_fusion
  12.7 1.9 fusion.3
  14.6 0.0 all-gather.2.cloned.1.call-update
  14.6 34.6 %all-gather.2.cloned.1.call-done = bf16[128,12288]{1,0:T(8,128)(2,1)} async-done(((bf16[128,1536]{1,0:T(8,128)(2,1)}), bf16[128,12288]{1,0:T(8,128)(2,1)}) %all-gather.2.cloned.1.call-update) | async-done | bytes 3145744 | tf_op jit(solution)/shard_map/all_gather | solution.py:64
  49.2 3.5 %copy.22 = bf16[128,12288]{0,1:T(8,128)(2,1)S(1)} copy(bf16[128,12288]{1,0:T(8,128)(2,1)} %all-gather.2.cloned.1.call-done) | data formatting | bytes 6291456 | tf_op jit(solution)/shard_map/all_gather | solution.py:64
  52.7 0.2 copy.23
  52.9 0.0 copy-start
  52.9 82.9 %all_to_all.31 = bf16[128,2,16,384]{0,3,1,2:T(8,128)(2,1)S(1)} all-to-all(bf16[128,2,16,384]{0,3,1,2:T(8,128)(2,1)S(1)} %copy.23), channel_id=1, replica_groups=mesh['arcs'=2,'trow'=8,'tcol'=16] {'tcol'}, dimensions={2} | all-to-all | bytes 6291456 | tf_op jit(solution)/shard_map/all_to_all | solution.py:68
  135.9 0.0 copy-done
  135.9 3.3 stack.2
  139.1 0.0 copy-start.2
  139.1 0.0 copy-start.1
  139.1 4.8 %all-to-all-start = ((bf16[16,128,1536]{2,1,0:T(8,128)(2,1)}), bf16[16,128,1536]{2,1,0:T(8,128)(2,1)}, u32[]{:S(2)}, u32[]{:S(2)}) async-start(bf16[16,128,1536]{2,1,0:T(8,128)(2,1)} %stack.2), calls=%async_computation | async-start | bytes 12582912 | tf_op jit(solution)/shard_map/all_to_all | solution.py:10
  143.9 0.0 copy-done.2
  143.9 0.7 convert_divide_fusion
  144.6 0.1 sub.25
  144.6 0.6 sub.26
  145.2 0.0 copy-done.1
  145.2 0.9 convolution_reduce_fusion
  146.2 3.7 %copy.24 = bf16[16,128,2,1,384]{1,0,4,2,3:T(8,128)(2,1)} copy(bf16[16,128,2,1,384]{1,4,2,0,3:T(8,128)(2,1)S(1)} %bitcast.28) | data formatting | bytes 6291456 | tf_op jit(solution)/shard_map/all_to_all | solution.py:68
  149.9 136.8 %all-to-all-done = bf16[16,128,1536]{2,1,0:T(8,128)(2,1)} async-done(((bf16[16,128,1536]{2,1,0:T(8,128)(2,1)}), bf16[16,128,1536]{2,1,0:T(8,128)(2,1)}, u32[]{:S(2)}, u32[]{:S(2)}) %all-to-all-start) | async-done | bytes 6291488 | tf_op jit(solution)/shard_map/all_to_all | solution.py:10
  286.6 0.8 broadcast_in_dim.2
  287.4 6.6 %all-to-all-start.3 = ((f32[32,1,1536]{2,1,0:T(1,128)}), f32[32,1,1536]{2,1,0:T(1,128)S(1)}, u32[]{:S(2)}, u32[]{:S(2)}) async-start(f32[32,1,1536]{2,1,0:T(1,128)} %broadcast_in_dim.2), calls=%async_computation.3 | async-start | bytes 393216 | tf_op jit(solution)/shard_map/all_to_all | solution.py:16
  294.1 9.5 %convolution_convert_fusion = bf16[1536,768]{0,1:T(8,128)(2,1)} fusion(bf16[2048,1536]{1,0:T(8,128)(2,1)} %bitcast.2, bf16[96,8,16,128]{3,2,1,0:T(8,128)(2,1)} %bitcast.30), kind=kOutput, calls=%fused_computation.1 | convolution fusion | flops 4833017856 | bytes 11796480 | tf_op jit(solution)/shard_map/dot_general | solution.py:36
  303.6 0.3 all-to-all-done.3
  303.9 3.8 %all-to-all-start.2 = ((bf16[2,1536,384]{1,2,0:T(8,128)(2,1)}), bf16[2,1536,384]{1,2,0:T(8,128)(2,1)S(1)}, u32[]{:S(2)}, u32[]{:S(2)}) async-start(bf16[2,1536,384]{1,2,0:T(8,128)(2,1)} %bitcast.31), calls=%async_computation.2 | async-start | bytes 4718592 | tf_op jit(solution)/shard_map/all_to_all | solution.py:31
  307.7 0.1 reduce_sum.39
  307.9 0.6 broadcast_multiply_fusion.1
  308.5 24.5 %all-to-all-done.2 = bf16[2,1536,384]{1,2,0:T(8,128)(2,1)S(1)} async-done(((bf16[2,1536,384]{1,2,0:T(8,128)(2,1)}), bf16[2,1536,384]{1,2,0:T(8,128)(2,1)S(1)}, u32[]{:S(2)}, u32[]{:S(2)}) %all-to-all-start.2) | async-done | bytes 2359328 | tf_op jit(solution)/shard_map/all_to_all | solution.py:31
  333.0 0.4 convert_reduce_fusion
  333.4 0.2 broadcast_multiply_fusion
  333.6 2.0 copy.26
Async XLA Ops:
  7.2 42.0 %all-gather.2.cloned.1.call-start = ((), (), s32[]{:S(2)}) async-start(), calls=%async_computation.4 | async-start | bytes 3538944 | tf_op jit(solution)/shard_map/all_gather | solution.py:64
  52.9 83.0 %copy-start = (bf16[128,1536]{1,0:T(8,128)(2,1)S(1)}, bf16[128,1536]{1,0:T(8,128)(2,1)}, u32[]{:S(2)}) copy-start(bf16[128,1536]{1,0:T(8,128)(2,1)} %fusion.3) | copy-start | bytes 1179652
  139.1 4.8 %copy-start.2 = (s32[4]{0:T(128)S(1)}, s32[4]{0:T(128)}, u32[]{:S(2)}) copy-start(s32[4]{0:T(128)} %param.6) | copy-start | bytes 52
  139.1 6.1 %copy-start.1 = (f32[128]{0:T(128)S(1)}, f32[128]{0:T(128)}, u32[]{:S(2)}) copy-start(f32[128]{0:T(128)} %param.5) | copy-start | bytes 1540
  139.1 147.5 %all-to-all-start = ((bf16[16,128,1536]{2,1,0:T(8,128)(2,1)}), bf16[16,128,1536]{2,1,0:T(8,128)(2,1)}, u32[]{:S(2)}, u32[]{:S(2)}) async-start(bf16[16,128,1536]{2,1,0:T(8,128)(2,1)} %stack.2), calls=%async_computation | async-start | bytes 12582912 | tf_op jit(solution)/shard_map/all_to_all | solution.py:10
  287.4 16.5 %all-to-all-start.3 = ((f32[32,1,1536]{2,1,0:T(1,128)}), f32[32,1,1536]{2,1,0:T(1,128)S(1)}, u32[]{:S(2)}, u32[]{:S(2)}) async-start(f32[32,1,1536]{2,1,0:T(1,128)} %broadcast_in_dim.2), calls=%async_computation.3 | async-start | bytes 393216 | tf_op jit(solution)/shard_map/all_to_all | solution.py:16
  303.9 29.1 %all-to-all-start.2 = ((bf16[2,1536,384]{1,2,0:T(8,128)(2,1)}), bf16[2,1536,384]{1,2,0:T(8,128)(2,1)S(1)}, u32[]{:S(2)}, u32[]{:S(2)}) async-start(bf16[2,1536,384]{1,2,0:T(8,128)(2,1)} %bitcast.31), calls=%async_computation.2 | async-start | bytes 4718592 | tf_op jit(solution)/shard_map/all_to_all | solution.py:31
Sparse Core Ops, SparseCore 0:
  14.7 34.4 all-gather.1
